TPU v7x, 128 devices: a whole 4x4x4 slice. The times are simulated.
128 devices in a mesh: emb: 8 (over x, core), seq: 16 (over z, y).
Axes of the slice: x: 4, y: 4, z: 4, core: 2. Of those that a mesh axis runs over, the one named last changes fastest.
Arguments:
- token_rows: int32 [8, 8192], P('emb', 'seq'), may hold values from 0 to 4607, as said below
- segment_ids: int32 [8, 8192], P('emb', 'seq'), may hold values from 0 to 3, never falling along the last dimension, each value on 1 to 4096 neighbouring positions
- requests: int32 [128, 128, 4], P(('emb', 'seq')), may hold values from 0 to 8191, as said below
- hot_table: bfloat16 [4096, 512], replicated, may hold values from -6 to 6
- cold_table: bfloat16 [1048576, 512], P(('emb', 'seq')), may hold values from -6 to 6
- input_weight: bfloat16 [512, 2048], replicated, may hold values from -0.75 to 0.75
- output_weight: bfloat16 [512, 512], replicated, may hold values from -0.25 to 0.25
- up_weight: bfloat16 [512, 2048], replicated, may hold values from -0.25 to 0.25
- down_weight: bfloat16 [2048, 512], replicated, may hold values from -0.125 to 0.125
Outputs:
- layer_output: bfloat16 [8, 8192, 512], P('emb', 'seq')
Inputs may be any that keep to these rules, and one draw needn't show every extreme that they name: `token_rows`: A value below 4096 names that row of hot_table. A value 4096 + o * 4 + k names slot k of the holding device's requests to owner o, and that slot is always a live one. Exactly 256 positions of each device name request slots. For each requesting device and owner the live requests fill slots 0 to c - 1, with c from 1 to 4; dead slots hold 0. Some owners, the same ones for all requesters, get all 4 slots live from every device, and every draw has at least one such owner. `segment_ids`: segment numbers never fall along a sequence.
All inputs are finite; a program needn't handle non-finite values.
Results may differ from a plain program's by a relative error of at most 0.0087.
Values may be sent and summed in bfloat16 or wider, within the bound.
A program may use at most 128 MiB of HBM per device.

v0:
```python
import math
import jax
import jax.numpy as jnp
from jax import lax
from jax.sharding import PartitionSpec as P

H = 16
epsilon = 1e-06


def in_order(pieces, dim):
    shape = list(pieces.shape[1:])
    shape[dim] *= pieces.shape[0]
    return jnp.moveaxis(pieces, 0, dim).reshape(shape)


def copy_for_each(value, axis):
    devices = lax.axis_size(axis)
    return lax.all_to_all(
        jnp.broadcast_to(value[None], (devices, *value.shape)), axis, 0, 0, tiled=True
    )


def collect(value, axis, dim):
    return in_order(copy_for_each(value, axis), dim)


def normalize(values):
    widened = values.astype(jnp.float32)
    return widened * lax.rsqrt(jnp.mean(widened * widened, axis=-1, keepdims=True) + epsilon)


def attend(queries, key_rows, value_rows, segments):
    length, groups, head_width = queries.shape
    block_rows = math.gcd(length, 2048)
    blocks = length // block_rows
    score_scale = 1.0 / math.sqrt(head_width)
    query_blocks = queries.reshape(blocks, block_rows, groups, head_width)
    key_blocks = key_rows.reshape(blocks, block_rows, groups, head_width)
    value_blocks = value_rows.reshape(blocks, block_rows, groups, head_width)
    segment_blocks = segments.reshape(blocks, block_rows)
    offsets = jnp.arange(block_rows, dtype=jnp.int32)

    def one_block(inputs):
        query_block, query_segments, position = inputs
        query_places = position * block_rows + offsets

        def add_keys(key_step, running):
            key_block = lax.dynamic_index_in_dim(key_blocks, key_step, 0, keepdims=False)
            value_block = lax.dynamic_index_in_dim(value_blocks, key_step, 0, keepdims=False)
            key_segments = lax.dynamic_index_in_dim(segment_blocks, key_step, 0, keepdims=False)
            key_places = key_step * block_rows + offsets
            scores = (
                jnp.einsum(
                    "qgc,kgc->gqk", query_block, key_block, preferred_element_type=jnp.float32
                )
                * score_scale
            )
            allowed = (key_places[None, :] <= query_places[:, None]) & (
                query_segments[:, None] == key_segments[None, :]
            )
            weights = jnp.where(allowed[None], jax.nn.silu(scores), 0.0).astype(jnp.bfloat16)
            return running + jnp.einsum(
                "gqk,kgc->qgc", weights, value_block, preferred_element_type=jnp.float32
            )

        running = lax.fori_loop(
            0, position + 1, add_keys, jnp.zeros((block_rows, groups, head_width), jnp.float32)
        )
        return running.astype(jnp.bfloat16)

    attended = lax.map(
        one_block, (query_blocks, segment_blocks, jnp.arange(blocks, dtype=jnp.int32))
    )
    return attended.reshape(length, groups, head_width)


def local(
    token_rows,
    segment_ids,
    requests,
    hot_table,
    cold_table,
    input_weight,
    output_weight,
    up_weight,
    down_weight,
):
    emb_devices = lax.axis_size("emb")
    seq_devices = lax.axis_size("seq")
    all_devices = emb_devices * seq_devices
    capacity = requests.shape[2]
    hot_count = hot_table.shape[0]
    model_width = hot_table.shape[1]
    tokens_here = token_rows.shape[1]
    head_groups = H // seq_devices
    head_width = model_width // H
    requested = requests[0]
    fetched = lax.all_to_all(
        cold_table[
            lax.all_to_all(requested, ("emb", "seq"), split_axis=0, concat_axis=0, tiled=True)
        ],
        ("emb", "seq"),
        split_axis=0,
        concat_axis=0,
        tiled=True,
    )
    fetched = fetched.reshape(all_devices * capacity, model_width)
    item_ids = token_rows[0]
    is_hot = item_ids < hot_count
    hot_rows = hot_table[jnp.where(is_hot, item_ids, 0)]
    cold_rows = fetched[jnp.where(is_hot, 0, item_ids - hot_count)]
    embedded = jnp.where(is_hot[:, None], hot_rows, cold_rows)
    normed_input = normalize(embedded).astype(jnp.bfloat16)
    grouped_weight = input_weight.reshape(model_width, seq_devices, head_groups, 4, head_width)
    segments = collect(segment_ids, "seq", 1)[0]
    gate_rounded = jnp.einsum(
        "td,dgec->gtec",
        normed_input,
        grouped_weight[:, :, :, 0, :],
        preferred_element_type=jnp.float32,
    ).astype(jnp.bfloat16)
    gate_units = jax.nn.silu(lax.optimization_barrier(gate_rounded).astype(jnp.float32))
    own_group = lax.axis_index("seq")
    own_weight = lax.dynamic_index_in_dim(grouped_weight, own_group, 1, keepdims=False)[
        :, :, 1:, :
    ].reshape(model_width, head_groups * 3 * head_width)
    gathered = jnp.dot(
        lax.all_gather(normed_input, "seq", axis=0, tiled=True),
        own_weight,
        preferred_element_type=jnp.float32,
    ).astype(jnp.bfloat16)
    head_rows = gathered.reshape(tokens_here * seq_devices, head_groups, 3, head_width)
    attended = attend(head_rows[:, :, 1], head_rows[:, :, 2], head_rows[:, :, 0], segments)
    returned = lax.all_to_all(
        attended.reshape(seq_devices, tokens_here * head_groups * head_width),
        "seq",
        split_axis=0,
        concat_axis=0,
        tiled=True,
    )
    returned = returned.reshape(seq_devices, tokens_here, head_groups, head_width).astype(
        jnp.float32
    )
    mean_square = jnp.mean(returned * returned, axis=(0, 2, 3))
    normed_heads = (
        returned * lax.rsqrt(mean_square + epsilon)[None, :, None, None] * gate_units
    ).astype(jnp.bfloat16)
    hidden = embedded.astype(jnp.float32) + jnp.einsum(
        "gtc,gcd->td",
        normed_heads.reshape(seq_devices, tokens_here, head_groups * head_width),
        output_weight.reshape(seq_devices, head_groups * head_width, model_width),
        preferred_element_type=jnp.float32,
    )
    normed_hidden = normalize(hidden).astype(jnp.bfloat16)
    activated = jax.nn.silu(
        jnp.dot(normed_hidden, up_weight, preferred_element_type=jnp.float32)
    ).astype(jnp.bfloat16)
    layer_output = (
        hidden + jnp.dot(activated, down_weight, preferred_element_type=jnp.float32)
    ).astype(jnp.bfloat16)
    return layer_output[None]


def solution(mesh):
    placed = (
        P("emb", "seq"),
        P("emb", "seq"),
        P(("emb", "seq"), None, None),
        P(),
        P(("emb", "seq"), None),
        P(),
        P(),
        P(),
        P(),
    )
    return jax.shard_map(
        local, mesh=mesh, in_specs=placed, out_specs=P("emb", "seq", None), check_vma=False
    )
```

profile of v0, /device:TPU:0, one launch (start us, length us, event | category | flops | bytes accessed | tf_op | source)
XLA Modules:
  0.0 304.7 jit_solution(13476258196587185154)
XLA Ops:
  6.5 0.9 copy.43
  7.5 20.5 %all_to_all.32 = s32[128,1,4]{2,1,0:T(1,128)S(1)} all-to-all(s32[128,1,4]{2,1,0:T(1,128)S(1)} %bitcast.141), channel_id=1, replica_groups=mesh['emb'=8,'seq'=16] {'emb','seq'}, dimensions={0} | all-to-all | bytes 4096 | tf_op jit(solution)/shard_map/all_to_all | solution.py:101
  28.1 6.4 %gather_fusion.1 = bf16[512,512]{1,0:T(8,128)(2,1)S(1)} fusion(bf16[8192,512]{1,0:T(8,128)(2,1)} %param.17, s32[1024]{0:T(1024)S(1)} %pad_clamp_fusion.1), kind=kCustom, calls=%fused_computation.1 | custom fusion | bytes 1050624 | tf_op jit(solution)/shard_map/gather | solution.py:100
  34.6 0.9 reshape.217
  35.5 5.7 %all-to-all-start.1 = ((bf16[128,4,512]{2,1,0:T(4,128)(2,1)}), bf16[128,4,512]{2,1,0:T(4,128)(2,1)}, u32[]{:S(2)}, u32[]{:S(2)}) async-start(bf16[128,4,512]{2,1,0:T(4,128)(2,1)} %reshape.217), calls=%async_computation.1 | async-start | bytes 1048576 | tf_op jit(solution)/shard_map/all_to_all | solution.py:99
  41.3 4.7 %gather_fusion = bf16[512,512]{1,0:T(8,128)(2,1)S(1)} fusion(bf16[4096,512]{1,0:T(8,128)(2,1)} %param.16, s32[1024]{0:T(1024)S(1)} %pad_clamp_fusion.2), kind=kCustom, calls=%fused_computation | custom fusion | bytes 1050624 | tf_op jit(solution)/shard_map/gather | solution.py:111
  46.3 8.1 %all-to-all-done.1 = bf16[128,4,512]{2,1,0:T(4,128)(2,1)} async-done(((bf16[128,4,512]{2,1,0:T(4,128)(2,1)}), bf16[128,4,512]{2,1,0:T(4,128)(2,1)}, u32[]{:S(2)}, u32[]{:S(2)}) %all-to-all-start.1) | async-done | bytes 524320 | tf_op jit(solution)/shard_map/all_to_all | solution.py:99
  54.4 1.2 reshape.200
  55.6 2.6 gather_fusion.2
  58.2 1.3 copy.45
  59.7 0.8 copy-done.2
  60.5 0.9 fusion.32
  61.4 0.6 broadcast_in_dim.52
  62.1 3.7 %all-to-all-start.2 = ((s32[16,1,512]{2,1,0:T(1,128)}), s32[16,1,512]{2,1,0:T(1,128)S(1)}, u32[]{:S(2)}, u32[]{:S(2)}) async-start(s32[16,1,512]{2,1,0:T(1,128)} %broadcast_in_dim.52), calls=%async_computation.2 | async-start | bytes 65536 | tf_op jit(solution)/shard_map/all_to_all | solution.py:19
  65.7 4.0 %copy.46 = bf16[512,2048]{0,1:T(8,128)(2,1)} copy(bf16[512,2048]{1,0:T(8,128)(2,1)} %param.18) | data formatting | bytes 4194304 | tf_op args[5]
  69.7 0.9 dynamic-slice_bitcast_fusion.1
  70.6 1.9 slice.30
  73.2 61.5 %all-gather.2.cloned.1.call-done = bf16[8192,512]{0,1:T(8,128)(2,1)} async-done(((bf16[512,512]{0,1:T(8,128)(2,1)}), bf16[8192,512]{0,1:T(8,128)(2,1)}) %all-gather.2.cloned.1.call-update) | async-done | bytes 8388624 | tf_op jit(solution)/shard_map/all_gather | solution.py:129
  134.7 4.8 %convolution_convert_fusion = bf16[8192,96]{0,1:T(8,128)(2,1)S(1)} fusion(bf16[512,96]{0,1:T(8,128)(2,1)S(1)} %bitcast.139, bf16[8192,512]{0,1:T(8,128)(2,1)} %all-gather.2.cloned.1.call-done), kind=kOutput, calls=%fused_computation.29 | convolution fusion | flops 806092800 | bytes 10059776 | tf_op jit(solution)/shard_map/dot_general | solution.py:128
  139.6 1.1 fusion.43
  140.7 1.2 reshape_squeeze.9
  141.9 1.3 copy.47
  143.2 2.2 reshape_squeeze.10
  145.4 2.1 copy.48
  147.5 2.2 reshape_squeeze.11
  149.8 2.1 copy.49
  151.9 93.7 %while.25 = (s32[]{:T(128)}, bf16[4,2048,1,32]{1,3,2,0:T(8,128)(2,1)}, s32[4]{0:T(128)S(1)}, bf16[4,2048,1,32]{1,3,2,0:T(8,128)(2,1)S(1)}, s32[4,2048]{1,0:T(4,1...) while((s32[]{:T(128)}, ...), condition=%wide.region_4.5_spmd.clone.clone, body=%wide.region_1.4_spmd.clone.clone.sunk | while | flops 578949120 | bytes 1934864 | solution.py:72
  151.9 0.6 dynamic_slice.55
  153.9 8.3 %while.26 = (s32[]{:T(128)}, f32[2048,1,32]{0,2,1:T(8,128)S(1)}, s32[]{:T(128)}, bf16[4,2048,1,32]{1,3,2,0:T(8,128)(2,1)}, s32[2048]{0:T(1024)S(1)}, /*index=5*/...) while((s32[]{:T(128)}, f32[2048,1,32]{0,2,1:T(8,128)S(1)}, ...), condition=%wide.region_3.3_spmd, body=%wide.region_2.2_spmd.sunk | while | flops 578881536 | bytes 984259 | solution.py:67
  154.0 8.2 %fusion.59 = f32[2048,1,32]{0,2,1:T(8,128)S(1)} fusion(f32[2048,1,32]{0,2,1:T(8,128)S(1)} %get-tuple-element.351, s32[2048]{0:T(1024)S(1)} %get-tuple-element.370, s32[2048]{0:T(1024)S(1)} %get-tuple-element.369, s32[2048]{0:T(1024)S(1)} %bitcast.134, s32[2048]{0:T(1024)S(1)} %broadcast_add_fusion.2, ...), kind=kOutput, calls=%fused_computation.13.clone.1 | convolution fusion | flops 578879488 | bytes 951296 | tf_op jit(solution)/shard_map/while/body/eval_jaxpr/while/body/gqk,kgc->qgc/dot_general | solution.py:63
  162.2 0.7 bitcast_dynamic-update-slice_fusion.2
  162.9 0.6 dynamic_slice.55
  164.9 16.6 %while.26 = (s32[]{:T(128)}, f32[2048,1,32]{0,2,1:T(8,128)S(1)}, s32[]{:T(128)}, bf16[4,2048,1,32]{1,3,2,0:T(8,128)(2,1)}, s32[2048]{0:T(1024)S(1)}, /*index=5*/...) while((s32[]{:T(128)}, f32[2048,1,32]{0,2,1:T(8,128)S(1)}, ...), condition=%wide.region_3.3_spmd, body=%wide.region_2.2_spmd.sunk | while | flops 578881536 | bytes 984259 | solution.py:67
  164.9 8.3 %fusion.59 = f32[2048,1,32]{0,2,1:T(8,128)S(1)} fusion(f32[2048,1,32]{0,2,1:T(8,128)S(1)} %get-tuple-element.351, s32[2048]{0:T(1024)S(1)} %get-tuple-element.370, s32[2048]{0:T(1024)S(1)} %get-tuple-element.369, s32[2048]{0:T(1024)S(1)} %bitcast.134, s32[2048]{0:T(1024)S(1)} %broadcast_add_fusion.2, ...), kind=kOutput, calls=%fused_computation.13.clone.1 | convolution fusion | flops 578879488 | bytes 951296 | tf_op jit(solution)/shard_map/while/body/eval_jaxpr/while/body/gqk,kgc->qgc/dot_general | solution.py:63
  173.3 8.2 %fusion.59 = f32[2048,1,32]{0,2,1:T(8,128)S(1)} fusion(f32[2048,1,32]{0,2,1:T(8,128)S(1)} %get-tuple-element.351, s32[2048]{0:T(1024)S(1)} %get-tuple-element.370, s32[2048]{0:T(1024)S(1)} %get-tuple-element.369, s32[2048]{0:T(1024)S(1)} %bitcast.134, s32[2048]{0:T(1024)S(1)} %broadcast_add_fusion.2, ...), kind=kOutput, calls=%fused_computation.13.clone.1 | convolution fusion | flops 578879488 | bytes 951296 | tf_op jit(solution)/shard_map/while/body/eval_jaxpr/while/body/gqk,kgc->qgc/dot_general | solution.py:63
  181.5 0.7 bitcast_dynamic-update-slice_fusion.2
  182.2 0.6 dynamic_slice.55
  184.2 24.9 %while.26 = (s32[]{:T(128)}, f32[2048,1,32]{0,2,1:T(8,128)S(1)}, s32[]{:T(128)}, bf16[4,2048,1,32]{1,3,2,0:T(8,128)(2,1)}, s32[2048]{0:T(1024)S(1)}, /*index=5*/...) while((s32[]{:T(128)}, f32[2048,1,32]{0,2,1:T(8,128)S(1)}, ...), condition=%wide.region_3.3_spmd, body=%wide.region_2.2_spmd.sunk | while | flops 578881536 | bytes 984259 | solution.py:67
  184.2 8.2 %fusion.59 = f32[2048,1,32]{0,2,1:T(8,128)S(1)} fusion(f32[2048,1,32]{0,2,1:T(8,128)S(1)} %get-tuple-element.351, s32[2048]{0:T(1024)S(1)} %get-tuple-element.370, s32[2048]{0:T(1024)S(1)} %get-tuple-element.369, s32[2048]{0:T(1024)S(1)} %bitcast.134, s32[2048]{0:T(1024)S(1)} %broadcast_add_fusion.2, ...), kind=kOutput, calls=%fused_computation.13.clone.1 | convolution fusion | flops 578879488 | bytes 951296 | tf_op jit(solution)/shard_map/while/body/eval_jaxpr/while/body/gqk,kgc->qgc/dot_general | solution.py:63
  192.5 8.2 %fusion.59 = f32[2048,1,32]{0,2,1:T(8,128)S(1)} fusion(f32[2048,1,32]{0,2,1:T(8,128)S(1)} %get-tuple-element.351, s32[2048]{0:T(1024)S(1)} %get-tuple-element.370, s32[2048]{0:T(1024)S(1)} %get-tuple-element.369, s32[2048]{0:T(1024)S(1)} %bitcast.134, s32[2048]{0:T(1024)S(1)} %broadcast_add_fusion.2, ...), kind=kOutput, calls=%fused_computation.13.clone.1 | convolution fusion | flops 578879488 | bytes 951296 | tf_op jit(solution)/shard_map/while/body/eval_jaxpr/while/body/gqk,kgc->qgc/dot_general | solution.py:63
  200.8 8.2 %fusion.59 = f32[2048,1,32]{0,2,1:T(8,128)S(1)} fusion(f32[2048,1,32]{0,2,1:T(8,128)S(1)} %get-tuple-element.351, s32[2048]{0:T(1024)S(1)} %get-tuple-element.370, s32[2048]{0:T(1024)S(1)} %get-tuple-element.369, s32[2048]{0:T(1024)S(1)} %bitcast.134, s32[2048]{0:T(1024)S(1)} %broadcast_add_fusion.2, ...), kind=kOutput, calls=%fused_computation.13.clone.1 | convolution fusion | flops 578879488 | bytes 951296 | tf_op jit(solution)/shard_map/while/body/eval_jaxpr/while/body/gqk,kgc->qgc/dot_general | solution.py:63
  209.1 0.7 bitcast_dynamic-update-slice_fusion.2
  209.8 0.6 dynamic_slice.55
  211.7 33.2 %while.26 = (s32[]{:T(128)}, f32[2048,1,32]{0,2,1:T(8,128)S(1)}, s32[]{:T(128)}, bf16[4,2048,1,32]{1,3,2,0:T(8,128)(2,1)}, s32[2048]{0:T(1024)S(1)}, /*index=5*/...) while((s32[]{:T(128)}, f32[2048,1,32]{0,2,1:T(8,128)S(1)}, ...), condition=%wide.region_3.3_spmd, body=%wide.region_2.2_spmd.sunk | while | flops 578881536 | bytes 984259 | solution.py:67
  211.8 8.2 %fusion.59 = f32[2048,1,32]{0,2,1:T(8,128)S(1)} fusion(f32[2048,1,32]{0,2,1:T(8,128)S(1)} %get-tuple-element.351, s32[2048]{0:T(1024)S(1)} %get-tuple-element.370, s32[2048]{0:T(1024)S(1)} %get-tuple-element.369, s32[2048]{0:T(1024)S(1)} %bitcast.134, s32[2048]{0:T(1024)S(1)} %broadcast_add_fusion.2, ...), kind=kOutput, calls=%fused_computation.13.clone.1 | convolution fusion | flops 578879488 | bytes 951296 | tf_op jit(solution)/shard_map/while/body/eval_jaxpr/while/body/gqk,kgc->qgc/dot_general | solution.py:63
  220.1 8.2 %fusion.59 = f32[2048,1,32]{0,2,1:T(8,128)S(1)} fusion(f32[2048,1,32]{0,2,1:T(8,128)S(1)} %get-tuple-element.351, s32[2048]{0:T(1024)S(1)} %get-tuple-element.370, s32[2048]{0:T(1024)S(1)} %get-tuple-element.369, s32[2048]{0:T(1024)S(1)} %bitcast.134, s32[2048]{0:T(1024)S(1)} %broadcast_add_fusion.2, ...), kind=kOutput, calls=%fused_computation.13.clone.1 | convolution fusion | flops 578879488 | bytes 951296 | tf_op jit(solution)/shard_map/while/body/eval_jaxpr/while/body/gqk,kgc->qgc/dot_general | solution.py:63
  228.4 8.2 %fusion.59 = f32[2048,1,32]{0,2,1:T(8,128)S(1)} fusion(f32[2048,1,32]{0,2,1:T(8,128)S(1)} %get-tuple-element.351, s32[2048]{0:T(1024)S(1)} %get-tuple-element.370, s32[2048]{0:T(1024)S(1)} %get-tuple-element.369, s32[2048]{0:T(1024)S(1)} %bitcast.134, s32[2048]{0:T(1024)S(1)} %broadcast_add_fusion.2, ...), kind=kOutput, calls=%fused_computation.13.clone.1 | convolution fusion | flops 578879488 | bytes 951296 | tf_op jit(solution)/shard_map/while/body/eval_jaxpr/while/body/gqk,kgc->qgc/dot_general | solution.py:63
  236.7 8.2 %fusion.59 = f32[2048,1,32]{0,2,1:T(8,128)S(1)} fusion(f32[2048,1,32]{0,2,1:T(8,128)S(1)} %get-tuple-element.351, s32[2048]{0:T(1024)S(1)} %get-tuple-element.370, s32[2048]{0:T(1024)S(1)} %get-tuple-element.369, s32[2048]{0:T(1024)S(1)} %bitcast.134, s32[2048]{0:T(1024)S(1)} %broadcast_add_fusion.2, ...), kind=kOutput, calls=%fused_computation.13.clone.1 | convolution fusion | flops 578879488 | bytes 951296 | tf_op jit(solution)/shard_map/while/body/eval_jaxpr/while/body/gqk,kgc->qgc/dot_general | solution.py:63
  245.0 0.7 bitcast_dynamic-update-slice_fusion.2
  245.6 2.7 copy.50
  248.4 5.4 %all_to_all.27 = bf16[16,1,16384]{2,1,0:T(2,128)(2,1)} reshape(bf16[4,2048,1,32]{3,1,0,2:T(8,128)(2,1)} %copy.50) | data formatting | bytes 1048576 | tf_op jit(solution)/shard_map/all_to_all | solution.py:135
  254.4 5.0 %reduce.9 = bf16[16,16384]{1,0:T(8,128)(2,1)S(1)} reduce(bf16[16,1,16384]{2,1,0:T(2,128)(2,1)} %all_to_all.27, bf16[]{:T(256)} %broadcast.198), dimensions={1}, to_apply=%all_to_all.27.reduce_sub_computation | reduce | bytes 1048578 | tf_op jit(solution)/shard_map/all_to_all | solution.py:135
  259.4 1.2 reshape.239
  260.5 4.9 %all-to-all-start.3 = ((bf16[16,2,8192]{2,1,0:T(2,128)(2,1)}), bf16[16,2,8192]{2,1,0:T(2,128)(2,1)S(1)}, u32[]{:S(2)}, u32[]{:S(2)}) async-start(bf16[16,2,8192]{2,1,0:T(2,128)(2,1)} %reshape.239), calls=%async_computation.3 | async-start | bytes 1048576 | tf_op jit(solution)/shard_map/all_to_all | solution.py:135
  265.5 1.5 fusion.44
  267.0 0.9 convert_bitcast_fusion
  267.9 7.9 %all-to-all-done.3 = bf16[16,2,8192]{2,1,0:T(2,128)(2,1)S(1)} async-done(((bf16[16,2,8192]{2,1,0:T(2,128)(2,1)}), bf16[16,2,8192]{2,1,0:T(2,128)(2,1)S(1)}, u32[]{:S(2)}, u32[]{:S(2)}) %all-to-all-start.3) | async-done | bytes 524320 | tf_op jit(solution)/shard_map/all_to_all | solution.py:135
  275.7 1.8 reshape.240
  277.5 4.7 %fusion.33 = (f32[16384]{0:T(1024)S(1)}, f32[16,16384]{1,0:T(8,128)S(1)}) fusion(bf16[16,1,16384]{2,1,0:T(2,128)(2,1)} %reshape.240), kind=kLoop, calls=%fused_computation.49 | loop fusion | flops 770048 | bytes 1638400 | tf_op jit(solution)/shard_map/reduce_sum | solution.py:145
  282.2 2.7 reshape.207
  284.9 3.7 %copy.52 = f32[16,512,1,32]{1,3,0,2:T(8,128)} copy(f32[16,512,1,32]{3,1,0,2:T(8,128)} %reshape.207) | data formatting | bytes 2097152 | tf_op jit(solution)/shard_map/convert_element_type | solution.py:142
  288.9 3.0 multiply_reduce_fusion
  291.9 5.0 %fusion.26 = bf16[1,512,512]{1,2,0:T(8,128)(2,1)S(1)} fusion(f32[512,512]{0,1:T(8,128)} %get-tuple-element.207, bf16[2048,512]{1,0:T(8,128)(2,1)S(1)} %copy-done, bf16[512,2048]{1,0:T(8,128)(2,1)} %param.20, f32[512]{0:T(512)S(1)} %add_rsqrt_fusion), kind=kOutput, calls=%fused_computation.40 | convolution fusion | flops 2153775104 | bytes 5769216 | tf_op jit(solution)/shard_map/dot_general | solution.py:160
  296.9 1.0 copy.56
  (76 shorter events, 2.6 us)
Async XLA Ops:
  6.5 285.4 %copy-start = (bf16[2048,512]{1,0:T(8,128)(2,1)S(1)}, bf16[2048,512]{1,0:T(8,128)(2,1)}, u32[]{:S(2)}) copy-start(bf16[2048,512]{1,0:T(8,128)(2,1)} %param.21) | copy-start | bytes 6291460
  6.5 34.7 %copy-start.5 = (s32[1,512]{1,0:T(1,128)S(1)}, s32[1,512]{1,0:T(1,128)}, u32[]{:S(2)}) copy-start(s32[1,512]{1,0:T(1,128)} %param.13) | copy-start | bytes 6148
  35.5 18.9 %all-to-all-start.1 = ((bf16[128,4,512]{2,1,0:T(4,128)(2,1)}), bf16[128,4,512]{2,1,0:T(4,128)(2,1)}, u32[]{:S(2)}, u32[]{:S(2)}) async-start(bf16[128,4,512]{2,1,0:T(4,128)(2,1)} %reshape.217), calls=%async_computation.1 | async-start | bytes 1048576 | tf_op jit(solution)/shard_map/all_to_all | solution.py:99
  41.2 93.5 %all-gather.2.cloned.1.call-start = ((), (), s32[]{:S(2)}) async-start(), calls=%async_computation.4 | async-start | bytes 8912896 | tf_op jit(solution)/shard_map/all_gather | solution.py:129
  55.6 5.9 %copy-start.6 = (s32[1,512]{1,0:T(1,128)S(1)}, s32[1,512]{1,0:T(1,128)}, u32[]{:S(2)}) copy-start(s32[1,512]{1,0:T(1,128)} %param.14) | copy-start | bytes 6148
  59.7 0.8 copy-start.2
  62.1 11.0 %all-to-all-start.2 = ((s32[16,1,512]{2,1,0:T(1,128)}), s32[16,1,512]{2,1,0:T(1,128)S(1)}, u32[]{:S(2)}, u32[]{:S(2)}) async-start(s32[16,1,512]{2,1,0:T(1,128)} %broadcast_in_dim.52), calls=%async_computation.2 | async-start | bytes 65536 | tf_op jit(solution)/shard_map/all_to_all | solution.py:19
  245.6 19.9 %copy-start.1 = (bf16[512,512]{0,1:T(8,128)(2,1)S(1)}, bf16[512,512]{0,1:T(8,128)(2,1)}, u32[]{:S(2)}) copy-start(bf16[512,512]{0,1:T(8,128)(2,1)} %fusion.32) | copy-start | bytes 1572868
  260.5 15.2 %all-to-all-start.3 = ((bf16[16,2,8192]{2,1,0:T(2,128)(2,1)}), bf16[16,2,8192]{2,1,0:T(2,128)(2,1)S(1)}, u32[]{:S(2)}, u32[]{:S(2)}) async-start(bf16[16,2,8192]{2,1,0:T(2,128)(2,1)} %reshape.239), calls=%async_computation.3 | async-start | bytes 1048576 | tf_op jit(solution)/shard_map/all_to_all | solution.py:135
  284.9 4.0 %copy-start.3 = (bf16[512,512]{0,1:T(8,128)(2,1)S(1)}, bf16[512,512]{0,1:T(8,128)(2,1)}, u32[]{:S(2)}) copy-start(bf16[512,512]{0,1:T(8,128)(2,1)} %copy-done.2) | copy-start | bytes 1572868
  284.9 4.0 %copy-start.4 = (bf16[16,512,1,32]{1,3,0,2:T(8,128)(2,1)S(1)}, bf16[16,512,1,32]{1,3,0,2:T(8,128)(2,1)}, u32[]{:S(2)}) copy-start(bf16[16,512,1,32]{1,3,0,2:T(8,128)(2,1)} %convert_bitcast_fusion) | copy-start | bytes 1572868
Sparse Core Ops, SparseCore 0:
  61.5 73.1 all-gather.1
where the time goes:
time: 306 us; the launch traced here: 305 us
  matrix products  96.7 us (32%)
  waiting for transfers between devices  78 us (25%)
  local copies, waits for them, and re-layouts  61.1 us (20%)
  blocking collectives  20.5 us (7%)
  other arithmetic  14.7 us (5%)
  starting transfers between devices  14.4 us (5%)
  between operations  13.6 us (4%)
  loops' own time  5.8 us (2%)
    dot_general x10, matrix products, add_keys(): jnp.einsum('gqk,kgc->qgc', weights, value_block, preferred_element_type=j...  82.4 us
    all_gather x1, waiting for transfers between devices, local(): lax.all_gather(normed_input, 'seq', axis=0, tiled=True)  61.5 us
    all_to_all x1, blocking collectives, local(): lax.all_to_all(requested, ('emb', 'seq'), split_axis=0, concat_axis=0, ti...  20.5 us
    unnamed x21, local copies, waits for them, and re-layouts  14.4 us
    all_to_all x1, waiting for transfers between devices, local(): lax.all_to_all(cold_table[lax.all_to_all(requested, ('emb', 'seq'), split...  8.09 us
    all_to_all x1, waiting for transfers between devices, local(): lax.all_to_all(attended.reshape(seq_devices, tokens_here * head_groups *...  7.86 us
    gather x2, local copies, waits for them, and re-layouts, local(): cold_table[lax.all_to_all(requested, ('emb', 'seq'), split_axis=0, concat...  7.36 us
    convert_element_type x2, local copies, waits for them, and re-layouts, local(): returned.reshape(seq_devices, tokens_here, head_groups, head_width)  6.41 us
  transfers between devices with their start and end apart: 4, of which 4 were waited for; matrix products, arithmetic and copies ran while one was open for 5% of the time, Pallas kernels for 0%

commit v1 on v0

--- a/solution.py
+++ b/solution.py
@@ -6,6 +6,11 @@
 
 H = 16
 epsilon = 1e-06
+
+
+def tiled_gather(array, axis, dim):
+    copies = jnp.concatenate([array] * lax.axis_size(axis), axis=dim)
+    return lax.all_to_all(copies, axis, dim, dim, tiled=True)
 
 
 def in_order(pieces, dim):
@@ -126,9 +131,7 @@
         :, :, 1:, :
     ].reshape(model_width, head_groups * 3 * head_width)
     gathered = jnp.dot(
-        lax.all_gather(normed_input, "seq", axis=0, tiled=True),
-        own_weight,
-        preferred_element_type=jnp.float32,
+        tiled_gather(normed_input, "seq", 0), own_weight, preferred_element_type=jnp.float32
     ).astype(jnp.bfloat16)
     head_rows = gathered.reshape(tokens_here * seq_devices, head_groups, 3, head_width)
     attended = attend(head_rows[:, :, 1], head_rows[:, :, 2], head_rows[:, :, 0], segments)

time: 306 us -> 396 us (1.29)
  waiting for transfers between devices: 78 us -> 143 us
  local copies, waits for them, and re-layouts: 61.1 us -> 84.3 us
  blocking collectives: 20.5 us -> 0 us
  starting transfers between devices: 14.4 us -> 33.6 us
  other arithmetic: 14.7 us -> 31.1 us
  between operations: 13.6 us -> 0.24 us
    all_to_all x0 -> x2, waiting for transfers between devices: none -> 125 us  [the longest x1 117 us: tiled_gather(): return lax.all_to_all(copies, axis, dim, dim, tiled=True)]
    all_gather x1 -> x0, waiting for transfers between devices: 61.5 us -> none  [local(): lax.all_gather(normed_input, 'seq', axis=0, tiled=True)]
    all_to_all x1 -> x0, blocking collectives: 20.5 us -> none  [local(): lax.all_to_all(requested, ('emb', 'seq'), split_axis=0, concat_axis=0, ti...]
    all_to_all x0 -> x2, local copies, waits for them, and re-layouts: none -> 19.8 us  [tiled_gather(): return lax.all_to_all(copies, axis, dim, dim, tiled=True)]
    all_to_all x0 -> x2, starting transfers between devices: none -> 18.4 us  [the longest x1 11.2 us: local(): lax.all_to_all(requested, ('emb', 'seq'), split_axis=0, concat_axis=0, ti...]
    unnamed x0 -> x15, other arithmetic: none -> 14 us
  transfers between devices with their start and end apart: 4 -> 5, of which waited for: 4 -> 4; matrix products, arithmetic and copies ran while one was open for 5% -> 11% of each run, Pallas kernels for 0% -> 0%
where the time goes in v1:
time: 396 us; the launch traced here: 394 us
  waiting for transfers between devices  143 us (36%)
  matrix products  96.8 us (24%)
  local copies, waits for them, and re-layouts  84.3 us (21%)
  starting transfers between devices  33.6 us (8%)
  other arithmetic  31.1 us (8%)
  loops' own time  5.78 us (1%)
    all_to_all x1, waiting for transfers between devices, tiled_gather(): return lax.all_to_all(copies, axis, dim, dim, tiled=True)  117 us
    dot_general x10, matrix products, add_keys(): jnp.einsum('gqk,kgc->qgc', weights, value_block, preferred_element_type=j...  82.4 us
    all_to_all x2, local copies, waits for them, and re-layouts, tiled_gather(): return lax.all_to_all(copies, axis, dim, dim, tiled=True)  19.8 us
    unnamed x21, local copies, waits for them, and re-layouts  16.8 us
    unnamed x15, other arithmetic  14 us
    all_to_all x1, starting transfers between devices, local(): lax.all_to_all(requested, ('emb', 'seq'), split_axis=0, concat_axis=0, ti...  11.2 us
    all_to_all x1, waiting for transfers between devices, local(): lax.all_to_all(attended.reshape(seq_devices, tokens_here * head_groups *...  9.79 us
    all_to_all x1, waiting for transfers between devices, local(): lax.all_to_all(requested, ('emb', 'seq'), split_axis=0, concat_axis=0, ti...  8.74 us
  transfers between devices with their start and end apart: 5, of which 4 were waited for; matrix products, arithmetic and copies ran while one was open for 11% of the time, Pallas kernels for 0%

profile of v1, /device:TPU:0, one launch (start us, length us, event | category | flops | bytes accessed | tf_op | source)
XLA Modules:
  0.0 394.4 jit_solution(15225239407448593968)
XLA Ops:
  0.0 1.6 copy.58
  1.6 11.2 %all-to-all-start = ((s32[128,1,4]{2,1,0:T(1,128)}), s32[128,1,4]{2,1,0:T(1,128)S(1)}, u32[]{:S(2)}, u32[]{:S(2)}) async-start(s32[128,1,4]{2,1,0:T(1,128)} %bitcast.9), calls=%async_computation | async-start | bytes 131072 | tf_op jit(solution)/shard_map/all_to_all | solution.py:106
  13.5 8.7 %all-to-all-done = s32[128,1,4]{2,1,0:T(1,128)S(1)} async-done(((s32[128,1,4]{2,1,0:T(1,128)}), s32[128,1,4]{2,1,0:T(1,128)S(1)}, u32[]{:S(2)}, u32[]{:S(2)}) %all-to-all-start) | async-done | bytes 2080 | tf_op jit(solution)/shard_map/all_to_all | solution.py:106
  22.3 6.4 %gather_fusion.1 = bf16[512,512]{1,0:T(8,128)(2,1)S(1)} fusion(bf16[8192,512]{1,0:T(8,128)(2,1)} %param.17, s32[1024]{0:T(1024)S(1)} %get-tuple-element.215), kind=kCustom, calls=%fused_computation.1 | custom fusion | bytes 1050624 | tf_op jit(solution)/shard_map/gather | solution.py:105
  29.7 5.7 %all-to-all-start.1 = ((bf16[128,4,512]{2,1,0:T(4,128)(2,1)}), bf16[128,4,512]{2,1,0:T(4,128)(2,1)}, u32[]{:S(2)}, u32[]{:S(2)}) async-start(bf16[128,4,512]{2,1,0:T(4,128)(2,1)} %reshape.219), calls=%async_computation.1 | async-start | bytes 1048576 | tf_op jit(solution)/shard_map/all_to_all | solution.py:104
  36.2 4.7 %gather_fusion = bf16[512,512]{1,0:T(8,128)(2,1)S(1)} fusion(bf16[4096,512]{1,0:T(8,128)(2,1)} %param.16, s32[1024]{0:T(1024)S(1)} %get-tuple-element.216), kind=kCustom, calls=%fused_computation | custom fusion | bytes 1050624 | tf_op jit(solution)/shard_map/gather | solution.py:116
  41.1 7.5 %all-to-all-done.1 = bf16[128,4,512]{2,1,0:T(4,128)(2,1)} async-done(((bf16[128,4,512]{2,1,0:T(4,128)(2,1)}), bf16[128,4,512]{2,1,0:T(4,128)(2,1)}, u32[]{:S(2)}, u32[]{:S(2)}) %all-to-all-start.1) | async-done | bytes 524320 | tf_op jit(solution)/shard_map/all_to_all | solution.py:104
  49.2 3.5 all-to-all-start.3
  52.7 1.2 reshape.202
  53.9 2.6 gather_fusion.2
  56.5 1.3 copy.60
  58.0 1.0 constant_dynamic-update-slice_fusion.15
  59.0 0.9 constant_dynamic-update-slice_fusion.14
  59.9 1.0 constant_dynamic-update-slice_fusion.13
  60.9 0.9 constant_dynamic-update-slice_fusion.12
  62.7 0.9 constant_dynamic-update-slice_fusion.10
  63.6 0.9 constant_dynamic-update-slice_fusion.9
  68.2 0.9 constant_dynamic-update-slice_fusion.4
  69.2 1.0 constant_dynamic-update-slice_fusion.3
  70.1 1.0 constant_dynamic-update-slice_fusion.2
  71.1 1.0 constant_dynamic-update-slice_fusion.1
  72.1 1.0 constant_dynamic-update-slice_fusion
  73.0 7.5 %copy.79 = bf16[64,16,8,512]{3,2,0,1:T(8,128)(2,1)} copy(bf16[64,16,8,512]{3,2,1,0:T(8,128)(2,1)} %bitcast.39) | data formatting | bytes 16777216 | tf_op jit(solution)/shard_map/all_to_all | solution.py:13
  80.5 7.2 %all-to-all-start.2 = ((bf16[16,512,512]{1,2,0:T(8,128)(2,1)}), bf16[16,512,512]{1,2,0:T(8,128)(2,1)}, u32[]{:S(2)}, u32[]{:S(2)}) async-start(bf16[16,512,512]{1,2,0:T(8,128)(2,1)} %bitcast.138), calls=%async_computation.2 | async-start | bytes 16777216 | tf_op jit(solution)/shard_map/all_to_all | solution.py:13
  87.8 3.9 %copy.63 = bf16[512,2048]{0,1:T(8,128)(2,1)} copy(bf16[512,2048]{1,0:T(8,128)(2,1)} %param.18) | data formatting | bytes 4194304 | tf_op args[5]
  91.7 1.9 slice.30
  94.7 116.6 %all-to-all-done.2 = bf16[16,512,512]{1,2,0:T(8,128)(2,1)} async-done(((bf16[16,512,512]{1,2,0:T(8,128)(2,1)}), bf16[16,512,512]{1,2,0:T(8,128)(2,1)}, u32[]{:S(2)}, u32[]{:S(2)}) %all-to-all-start.2) | async-done | bytes 8388640 | tf_op jit(solution)/shard_map/all_to_all | solution.py:13
  211.3 12.3 %copy.62 = bf16[16,512,512]{2,1,0:T(8,128)(2,1)} copy(bf16[16,512,512]{1,2,0:T(8,128)(2,1)} %all-to-all-done.2) | data formatting | bytes 16777216 | tf_op jit(solution)/shard_map/all_to_all | solution.py:13
  223.6 6.0 %convolution_convert_fusion = bf16[8192,96]{0,1:T(8,128)(2,1)S(1)} fusion(bf16[8192,512]{1,0:T(8,128)(2,1)} %bitcast.137, bf16[512,96]{0,1:T(8,128)(2,1)S(1)} %bitcast.145), kind=kOutput, calls=%fused_computation.29 | convolution fusion | flops 806092800 | bytes 10059776 | tf_op jit(solution)/shard_map/dot_general | solution.py:133
  229.6 1.1 fusion.45
  230.7 1.2 reshape_squeeze.9
  231.9 1.3 copy.64
  233.2 2.2 reshape_squeeze.10
  235.5 2.1 copy.65
  237.6 2.2 reshape_squeeze.11
  239.8 2.1 copy.66
  241.9 93.8 %while.25 = (s32[]{:T(128)}, bf16[4,2048,1,32]{1,3,2,0:T(8,128)(2,1)}, s32[4]{0:T(128)S(1)}, bf16[4,2048,1,32]{1,3,2,0:T(8,128)(2,1)S(1)}, s32[4,2048]{1,0:T(4,1...) while((s32[]{:T(128)}, ...), condition=%wide.region_4.5_spmd.clone.clone, body=%wide.region_1.4_spmd.clone.clone.sunk | while | flops 578949120 | bytes 1935356 | solution.py:77
  244.0 8.3 %while.26 = (s32[]{:T(128)}, f32[2048,1,32]{0,2,1:T(8,128)S(1)}, s32[]{:T(128)}, bf16[4,2048,1,32]{1,3,2,0:T(8,128)(2,1)}, s32[2048]{0:T(1024)S(1)}, /*index=5*/...) while((s32[]{:T(128)}, f32[2048,1,32]{0,2,1:T(8,128)S(1)}, ...), condition=%wide.region_3.3_spmd, body=%wide.region_2.2_spmd.sunk | while | flops 578881536 | bytes 984251 | solution.py:72
  244.0 8.2 %fusion.59 = f32[2048,1,32]{0,2,1:T(8,128)S(1)} fusion(f32[2048,1,32]{0,2,1:T(8,128)S(1)} %get-tuple-element.360, s32[2048]{0:T(1024)S(1)} %get-tuple-element.379, s32[2048]{0:T(1024)S(1)} %get-tuple-element.378, s32[2048]{0:T(1024)S(1)} %bitcast.140, s32[2048]{0:T(1024)S(1)} %broadcast_add_fusion.2, ...), kind=kOutput, calls=%fused_computation.13.clone.1 | convolution fusion | flops 578879488 | bytes 951296 | tf_op jit(solution)/shard_map/while/body/eval_jaxpr/while/body/gqk,kgc->qgc/dot_general | solution.py:68
  255.0 16.6 %while.26 = (s32[]{:T(128)}, f32[2048,1,32]{0,2,1:T(8,128)S(1)}, s32[]{:T(128)}, bf16[4,2048,1,32]{1,3,2,0:T(8,128)(2,1)}, s32[2048]{0:T(1024)S(1)}, /*index=5*/...) while((s32[]{:T(128)}, f32[2048,1,32]{0,2,1:T(8,128)S(1)}, ...), condition=%wide.region_3.3_spmd, body=%wide.region_2.2_spmd.sunk | while | flops 578881536 | bytes 984251 | solution.py:72
  255.0 8.2 %fusion.59 = f32[2048,1,32]{0,2,1:T(8,128)S(1)} fusion(f32[2048,1,32]{0,2,1:T(8,128)S(1)} %get-tuple-element.360, s32[2048]{0:T(1024)S(1)} %get-tuple-element.379, s32[2048]{0:T(1024)S(1)} %get-tuple-element.378, s32[2048]{0:T(1024)S(1)} %bitcast.140, s32[2048]{0:T(1024)S(1)} %broadcast_add_fusion.2, ...), kind=kOutput, calls=%fused_computation.13.clone.1 | convolution fusion | flops 578879488 | bytes 951296 | tf_op jit(solution)/shard_map/while/body/eval_jaxpr/while/body/gqk,kgc->qgc/dot_general | solution.py:68
  263.3 8.2 %fusion.59 = f32[2048,1,32]{0,2,1:T(8,128)S(1)} fusion(f32[2048,1,32]{0,2,1:T(8,128)S(1)} %get-tuple-element.360, s32[2048]{0:T(1024)S(1)} %get-tuple-element.379, s32[2048]{0:T(1024)S(1)} %get-tuple-element.378, s32[2048]{0:T(1024)S(1)} %bitcast.140, s32[2048]{0:T(1024)S(1)} %broadcast_add_fusion.2, ...), kind=kOutput, calls=%fused_computation.13.clone.1 | convolution fusion | flops 578879488 | bytes 951296 | tf_op jit(solution)/shard_map/while/body/eval_jaxpr/while/body/gqk,kgc->qgc/dot_general | solution.py:68
  274.3 24.9 %while.26 = (s32[]{:T(128)}, f32[2048,1,32]{0,2,1:T(8,128)S(1)}, s32[]{:T(128)}, bf16[4,2048,1,32]{1,3,2,0:T(8,128)(2,1)}, s32[2048]{0:T(1024)S(1)}, /*index=5*/...) while((s32[]{:T(128)}, f32[2048,1,32]{0,2,1:T(8,128)S(1)}, ...), condition=%wide.region_3.3_spmd, body=%wide.region_2.2_spmd.sunk | while | flops 578881536 | bytes 984251 | solution.py:72
  274.3 8.2 %fusion.59 = f32[2048,1,32]{0,2,1:T(8,128)S(1)} fusion(f32[2048,1,32]{0,2,1:T(8,128)S(1)} %get-tuple-element.360, s32[2048]{0:T(1024)S(1)} %get-tuple-element.379, s32[2048]{0:T(1024)S(1)} %get-tuple-element.378, s32[2048]{0:T(1024)S(1)} %bitcast.140, s32[2048]{0:T(1024)S(1)} %broadcast_add_fusion.2, ...), kind=kOutput, calls=%fused_computation.13.clone.1 | convolution fusion | flops 578879488 | bytes 951296 | tf_op jit(solution)/shard_map/while/body/eval_jaxpr/while/body/gqk,kgc->qgc/dot_general | solution.py:68
  282.6 8.2 %fusion.59 = f32[2048,1,32]{0,2,1:T(8,128)S(1)} fusion(f32[2048,1,32]{0,2,1:T(8,128)S(1)} %get-tuple-element.360, s32[2048]{0:T(1024)S(1)} %get-tuple-element.379, s32[2048]{0:T(1024)S(1)} %get-tuple-element.378, s32[2048]{0:T(1024)S(1)} %bitcast.140, s32[2048]{0:T(1024)S(1)} %broadcast_add_fusion.2, ...), kind=kOutput, calls=%fused_computation.13.clone.1 | convolution fusion | flops 578879488 | bytes 951296 | tf_op jit(solution)/shard_map/while/body/eval_jaxpr/while/body/gqk,kgc->qgc/dot_general | solution.py:68
  290.9 8.2 %fusion.59 = f32[2048,1,32]{0,2,1:T(8,128)S(1)} fusion(f32[2048,1,32]{0,2,1:T(8,128)S(1)} %get-tuple-element.360, s32[2048]{0:T(1024)S(1)} %get-tuple-element.379, s32[2048]{0:T(1024)S(1)} %get-tuple-element.378, s32[2048]{0:T(1024)S(1)} %bitcast.140, s32[2048]{0:T(1024)S(1)} %broadcast_add_fusion.2, ...), kind=kOutput, calls=%fused_computation.13.clone.1 | convolution fusion | flops 578879488 | bytes 951296 | tf_op jit(solution)/shard_map/while/body/eval_jaxpr/while/body/gqk,kgc->qgc/dot_general | solution.py:68
  301.9 33.2 %while.26 = (s32[]{:T(128)}, f32[2048,1,32]{0,2,1:T(8,128)S(1)}, s32[]{:T(128)}, bf16[4,2048,1,32]{1,3,2,0:T(8,128)(2,1)}, s32[2048]{0:T(1024)S(1)}, /*index=5*/...) while((s32[]{:T(128)}, f32[2048,1,32]{0,2,1:T(8,128)S(1)}, ...), condition=%wide.region_3.3_spmd, body=%wide.region_2.2_spmd.sunk | while | flops 578881536 | bytes 984251 | solution.py:72
  301.9 8.2 %fusion.59 = f32[2048,1,32]{0,2,1:T(8,128)S(1)} fusion(f32[2048,1,32]{0,2,1:T(8,128)S(1)} %get-tuple-element.360, s32[2048]{0:T(1024)S(1)} %get-tuple-element.379, s32[2048]{0:T(1024)S(1)} %get-tuple-element.378, s32[2048]{0:T(1024)S(1)} %bitcast.140, s32[2048]{0:T(1024)S(1)} %broadcast_add_fusion.2, ...), kind=kOutput, calls=%fused_computation.13.clone.1 | convolution fusion | flops 578879488 | bytes 951296 | tf_op jit(solution)/shard_map/while/body/eval_jaxpr/while/body/gqk,kgc->qgc/dot_general | solution.py:68
  310.2 8.2 %fusion.59 = f32[2048,1,32]{0,2,1:T(8,128)S(1)} fusion(f32[2048,1,32]{0,2,1:T(8,128)S(1)} %get-tuple-element.360, s32[2048]{0:T(1024)S(1)} %get-tuple-element.379, s32[2048]{0:T(1024)S(1)} %get-tuple-element.378, s32[2048]{0:T(1024)S(1)} %bitcast.140, s32[2048]{0:T(1024)S(1)} %broadcast_add_fusion.2, ...), kind=kOutput, calls=%fused_computation.13.clone.1 | convolution fusion | flops 578879488 | bytes 951296 | tf_op jit(solution)/shard_map/while/body/eval_jaxpr/while/body/gqk,kgc->qgc/dot_general | solution.py:68
  318.5 8.2 %fusion.59 = f32[2048,1,32]{0,2,1:T(8,128)S(1)} fusion(f32[2048,1,32]{0,2,1:T(8,128)S(1)} %get-tuple-element.360, s32[2048]{0:T(1024)S(1)} %get-tuple-element.379, s32[2048]{0:T(1024)S(1)} %get-tuple-element.378, s32[2048]{0:T(1024)S(1)} %bitcast.140, s32[2048]{0:T(1024)S(1)} %broadcast_add_fusion.2, ...), kind=kOutput, calls=%fused_computation.13.clone.1 | convolution fusion | flops 578879488 | bytes 951296 | tf_op jit(solution)/shard_map/while/body/eval_jaxpr/while/body/gqk,kgc->qgc/dot_general | solution.py:68
  326.8 8.2 %fusion.59 = f32[2048,1,32]{0,2,1:T(8,128)S(1)} fusion(f32[2048,1,32]{0,2,1:T(8,128)S(1)} %get-tuple-element.360, s32[2048]{0:T(1024)S(1)} %get-tuple-element.379, s32[2048]{0:T(1024)S(1)} %get-tuple-element.378, s32[2048]{0:T(1024)S(1)} %bitcast.140, s32[2048]{0:T(1024)S(1)} %broadcast_add_fusion.2, ...), kind=kOutput, calls=%fused_computation.13.clone.1 | convolution fusion | flops 578879488 | bytes 951296 | tf_op jit(solution)/shard_map/while/body/eval_jaxpr/while/body/gqk,kgc->qgc/dot_general | solution.py:68
  335.8 2.8 copy.67
  338.6 5.4 %all_to_all.38 = bf16[16,1,16384]{2,1,0:T(2,128)(2,1)} reshape(bf16[4,2048,1,32]{3,1,0,2:T(8,128)(2,1)} %copy.67) | data formatting | bytes 1048576 | tf_op jit(solution)/shard_map/all_to_all | solution.py:138
  344.5 5.7 %reduce.9 = bf16[16,16384]{1,0:T(8,128)(2,1)} reduce(bf16[16,1,16384]{2,1,0:T(2,128)(2,1)} %all_to_all.38, bf16[]{:T(256)} %broadcast.198), dimensions={1}, to_apply=%all_to_all.38.reduce_sub_computation | reduce | bytes 1048578 | tf_op jit(solution)/shard_map/all_to_all | solution.py:138
  350.2 2.2 reshape.241
  352.4 6.0 %all-to-all-start.4 = ((bf16[16,2,8192]{2,1,0:T(2,128)(2,1)}), bf16[16,2,8192]{2,1,0:T(2,128)(2,1)}, u32[]{:S(2)}, u32[]{:S(2)}) async-start(bf16[16,2,8192]{2,1,0:T(2,128)(2,1)} %reshape.241), calls=%async_computation.4 | async-start | bytes 1048576 | tf_op jit(solution)/shard_map/all_to_all | solution.py:138
  358.9 9.8 %all-to-all-done.4 = bf16[16,2,8192]{2,1,0:T(2,128)(2,1)} async-done(((bf16[16,2,8192]{2,1,0:T(2,128)(2,1)}), bf16[16,2,8192]{2,1,0:T(2,128)(2,1)}, u32[]{:S(2)}, u32[]{:S(2)}) %all-to-all-start.4) | async-done | bytes 524320 | tf_op jit(solution)/shard_map/all_to_all | solution.py:138
  368.7 3.5 reshape.242
  372.2 5.6 %fusion.33 = (f32[16384]{0:T(1024)S(1)}, f32[16,16384]{1,0:T(8,128)}) fusion(bf16[16,1,16384]{2,1,0:T(2,128)(2,1)} %reshape.242), kind=kLoop, calls=%fused_computation.50 | loop fusion | flops 770048 | bytes 1638400 | tf_op jit(solution)/shard_map/reduce_sum | solution.py:148
  377.8 3.7 reshape.209
  381.6 3.6 copy.69
  385.5 3.0 multiply_reduce_fusion
  388.5 5.0 %fusion.26 = bf16[1,512,512]{1,2,0:T(8,128)(2,1)S(1)} fusion(f32[512,512]{0,1:T(8,128)} %get-tuple-element.214, bf16[2048,512]{1,0:T(8,128)(2,1)S(1)} %copy-done, bf16[512,2048]{1,0:T(8,128)(2,1)} %param.20, f32[512]{0:T(512)S(1)} %add_rsqrt_fusion), kind=kOutput, calls=%fused_computation.41 | convolution fusion | flops 2153775104 | bytes 5769216 | tf_op jit(solution)/shard_map/dot_general | solution.py:163
  393.4 1.0 copy.73
  (92 shorter events, 16.1 us)
Async XLA Ops:
  0.0 388.5 %copy-start = (bf16[2048,512]{1,0:T(8,128)(2,1)S(1)}, bf16[2048,512]{1,0:T(8,128)(2,1)}, u32[]{:S(2)}) copy-start(bf16[2048,512]{1,0:T(8,128)(2,1)} %param.21) | copy-start | bytes 6291460
  0.0 48.6 %copy-start.6 = (s32[1,512]{1,0:T(1,128)S(1)}, s32[1,512]{1,0:T(1,128)}, u32[]{:S(2)}) copy-start(s32[1,512]{1,0:T(1,128)} %param.14) | copy-start | bytes 6148
  1.6 20.6 %all-to-all-start = ((s32[128,1,4]{2,1,0:T(1,128)}), s32[128,1,4]{2,1,0:T(1,128)S(1)}, u32[]{:S(2)}, u32[]{:S(2)}) async-start(s32[128,1,4]{2,1,0:T(1,128)} %bitcast.9), calls=%async_computation | async-start | bytes 131072 | tf_op jit(solution)/shard_map/all_to_all | solution.py:106
  29.7 18.9 %all-to-all-start.1 = ((bf16[128,4,512]{2,1,0:T(4,128)(2,1)}), bf16[128,4,512]{2,1,0:T(4,128)(2,1)}, u32[]{:S(2)}, u32[]{:S(2)}) async-start(bf16[128,4,512]{2,1,0:T(4,128)(2,1)} %reshape.219), calls=%async_computation.1 | async-start | bytes 1048576 | tf_op jit(solution)/shard_map/all_to_all | solution.py:104
  49.2 31.3 %all-to-all-start.3 = ((s32[16,1,512]{2,1,0:T(1,128)}), s32[16,1,512]{2,1,0:T(1,128)S(1)}, u32[]{:S(2)}, u32[]{:S(2)}) async-start(s32[16,1,512]{2,1,0:T(1,128)} %broadcast_in_dim.52), calls=%async_computation.3 | async-start | bytes 65536 | tf_op jit(solution)/shard_map/all_to_all | solution.py:24
  58.0 15.0 %copy-start.1 = (bf16[512,512]{0,1:T(8,128)(2,1)}, bf16[512,512]{0,1:T(8,128)(2,1)S(1)}, u32[]{:S(2)}) copy-start(bf16[512,512]{0,1:T(8,128)(2,1)S(1)} %get-tuple-element.207) | copy-start | bytes 1572868
  58.0 15.0 %copy-start.4 = (f32[512]{0:T(512)}, f32[512]{0:T(512)S(1)}, u32[]{:S(2)}) copy-start(f32[512]{0:T(512)S(1)} %add_rsqrt_fusion.2) | copy-start | bytes 6148
  80.5 130.7 %all-to-all-start.2 = ((bf16[16,512,512]{1,2,0:T(8,128)(2,1)}), bf16[16,512,512]{1,2,0:T(8,128)(2,1)}, u32[]{:S(2)}, u32[]{:S(2)}) async-start(bf16[16,512,512]{1,2,0:T(8,128)(2,1)} %bitcast.138), calls=%async_computation.2 | async-start | bytes 16777216 | tf_op jit(solution)/shard_map/all_to_all | solution.py:13
  335.8 22.6 %copy-start.2 = (bf16[512,512]{0,1:T(8,128)(2,1)S(1)}, bf16[512,512]{0,1:T(8,128)(2,1)}, u32[]{:S(2)}) copy-start(bf16[512,512]{0,1:T(8,128)(2,1)} %copy-done.1) | copy-start | bytes 1572868
  335.8 22.6 %copy-start.3 = (bf16[512,16,1,1,32]{0,4,3,1,2:T(8,128)(2,1)S(1)}, bf16[512,16,1,1,32]{0,4,3,1,2:T(8,128)(2,1)}, u32[]{:S(2)}) copy-start(bf16[512,16,1,1,32]{0,4,3,1,2:T(8,128)(2,1)} %slice.30) | copy-start | bytes 1572868
  335.8 22.6 %copy-start.5 = (f32[512]{0:T(512)S(1)}, f32[512]{0:T(512)}, u32[]{:S(2)}) copy-start(f32[512]{0:T(512)} %copy-done.4) | copy-start | bytes 6148
  352.4 16.3 %all-to-all-start.4 = ((bf16[16,2,8192]{2,1,0:T(2,128)(2,1)}), bf16[16,2,8192]{2,1,0:T(2,128)(2,1)}, u32[]{:S(2)}, u32[]{:S(2)}) async-start(bf16[16,2,8192]{2,1,0:T(2,128)(2,1)} %reshape.241), calls=%async_computation.4 | async-start | bytes 1048576 | tf_op jit(solution)/shard_map/all_to_all | solution.py:138
